TPU v7x, 128 devices: a whole 4x4x4 slice. The times are simulated.
128 devices in a mesh: sub: 128 (over y, z, x, core).
Axes of the slice: x: 4, y: 4, z: 4, core: 2. Of those that a mesh axis runs over, the one named last changes fastest.
Arguments:
- right_side: float32 [512, 128, 512], P('sub'), may hold values from -8 to 8
- sigma: float32 [512, 128, 512], P('sub'), may hold values from 0.25 to 2
- wind: float32 [512, 128, 512], P('sub'), may hold values from -0.8 to 0.8
- local_inverse: float32 [128, 512, 512], P('sub'), may hold values from -1 to 2, as said below
- basis_y: float32 [128, 32], replicated, may hold values from -0.5 to 0.5
- basis_z: float32 [512, 64], replicated, may hold values from -0.25 to 0.25
- gamma: float32 [7, 32, 64], replicated, may hold values from 0.3 to 3
Outputs:
- solution_field: float32 [512, 128, 512], P('sub')
- residual: float32 [512, 128, 512], P('sub')
Inputs may be any that keep to these rules, and one draw needn't show every extreme that they name: `local_inverse`: each block is the identity plus a perturbation whose entries lie within 2/sqrt(512) of zero; each row of the perturbation has norm about one half.
All inputs are finite; a program needn't handle non-finite values.
Results may differ from a plain program's by a relative error of at most 0.00022.
Values sent between devices are 32-bit elements; how exact they have to be, the bound alone decides.
A program may use at most 64 MiB of HBM per device.

v0:
```python
import jax
import jax.numpy as jnp
from jax import lax
from jax.sharding import Mesh
from jax.sharding import PartitionSpec as P

SUB = ("sub_0", "sub_1", "sub_2", "sub_3")


HIGH = lax.Precision.HIGHEST


def extended(cells, sides, width):
    for axis, dim in sides:
        count = lax.axis_size(axis)
        ends = count - 1
        head = lax.slice_in_dim(cells, 0, width, axis=dim)
        tail = lax.slice_in_dim(cells, cells.shape[dim] - width, cells.shape[dim], axis=dim)
        cells = jnp.concatenate(
            [
                lax.ppermute(tail, axis, [(i, (i + 1) % count) for i in range(ends)]),
                cells,
                lax.ppermute(head, axis, [((i + 1) % count, i) for i in range(ends)]),
            ],
            axis=dim,
        )
    return cells


def swapped(block, axis, apart):
    count = lax.axis_size(axis)
    route = []
    for low in range(count):
        high = low | 1 << apart
        if high != low and high < count:
            route += [(low, high), (high, low)]
    return lax.ppermute(block, axis, route)


def one_axis_at_a_time(shard, axes):
    for axis in axes:
        shard = lax.psum(shard, axis)
    return shard


def apply_operator(field, sigma, wind):
    padded_x = extended(field, ((SUB, 0),), 1)
    upper = padded_x[2:]
    lower = padded_x[:-2]
    padded_y = jnp.pad(field, ((0, 0), (1, 1), (0, 0)))
    padded_z = jnp.pad(field, ((0, 0), (0, 0), (1, 1)))
    beside = (
        upper
        + lower
        + padded_y[:, 2:]
        + padded_y[:, :-2]
        + padded_z[:, :, 2:]
        + padded_z[:, :, :-2]
    )
    return (6.0 + sigma) * field - beside + wind * (upper - lower)


def precondition(field, local_inverse, basis_y, basis_z, gamma):
    layers, rows, depth = field.shape
    local = jnp.dot(field.reshape(layers * rows, depth), local_inverse[0], precision=HIGH).reshape(
        layers, rows, depth
    )
    summed = jnp.sum(field, axis=0)
    proj = jnp.dot(basis_y.T, jnp.dot(summed, basis_z, precision=HIGH), precision=HIGH)
    levels = lax.axis_size(SUB).bit_length() - 1
    coarse = jnp.zeros_like(proj)
    for level in range(levels):
        partial_sum = proj
        for which in range(level + 1):
            partial_sum = partial_sum + swapped(partial_sum, SUB, which)
        coarse = coarse + gamma[level] * partial_sum / jnp.sqrt(
            jnp.float32(layers * 2 ** (level + 1))
        )
    spread = jnp.dot(basis_y, jnp.dot(coarse, basis_z.T, precision=HIGH), precision=HIGH)
    return local + spread[None]


def orthogonal_step(image, vectors):
    products = [jnp.sum(vector * image) for vector in vectors]
    sums = one_axis_at_a_time(jnp.stack(products + [jnp.sum(image * image)]), SUB)
    squares = sums[len(vectors)]
    for index in range(len(vectors)):
        image = image - sums[index] * vectors[index]
        squares = squares - sums[index] * sums[index]
    length = jnp.sqrt(squares)
    return (sums, image, length)


def on_device(right_side, sigma, wind, local_inverse, basis_y, basis_z, gamma):
    beta = jnp.sqrt(one_axis_at_a_time(jnp.sum(right_side * right_side), SUB))
    first = right_side / beta
    z_one = precondition(first, local_inverse, basis_y, basis_z, gamma)
    image = apply_operator(z_one, sigma, wind)
    sums, image, h21 = orthogonal_step(image, [first])
    h11 = sums[0]
    second = image / h21
    z_two = precondition(second, local_inverse, basis_y, basis_z, gamma)
    image = apply_operator(z_two, sigma, wind)
    sums, image, h32 = orthogonal_step(image, [first, second])
    h12 = sums[0]
    h22 = sums[1]
    m11 = h11 * h11 + h21 * h21
    m12 = h11 * h12 + h21 * h22
    m22 = h12 * h12 + h22 * h22 + h32 * h32
    q_one = h11 * beta
    q_two = h12 * beta
    determ = m11 * m22 - m12 * m12
    y_one = (m22 * q_one - m12 * q_two) / determ
    y_two = (m11 * q_two - m12 * q_one) / determ
    solution_field = y_one * z_one + y_two * z_two
    residual = right_side - apply_operator(solution_field, sigma, wind)
    return (solution_field, residual)


def solution(mesh):
    torus = Mesh(mesh.devices.reshape(4, 4, 4, 2), ("sub_0", "sub_1", "sub_2", "sub_3"))
    in_specs = (
        P(SUB, None, None),
        P(SUB, None, None),
        P(SUB, None, None),
        P(SUB, None, None),
        P(),
        P(),
        P(),
    )
    out_specs = (P(SUB, None, None), P(SUB, None, None))
    return jax.shard_map(
        on_device, mesh=torus, in_specs=in_specs, out_specs=out_specs, check_vma=False
    )
```

profile of v0, /device:TPU:8, one launch (start us, length us, event | category | flops | bytes accessed | tf_op | source)
XLA Modules:
  0.0 226.4 jit_solution(10502179477311217796)
XLA Ops:
  0.7 2.2 multiply_reduce_fusion.5
  2.9 9.3 %psum.84 = f32[]{:T(128)} all-reduce(f32[]{:T(128)} %multiply_reduce_fusion.5), channel_id=1, replica_groups=mesh['sub_0'=4,'sub_1'=4,'sub_2'=4,'sub_3'=2] {'sub_0'}, use_global_device_ids=true, to_apply=%region_1.0 | all-reduce | flops 1 | bytes 8 | tf_op jit(solution)/shard_map/psum | solution.py:42
  12.2 12.4 %psum.85 = f32[]{:T(128)} all-reduce(f32[]{:T(128)} %psum.84), channel_id=1, replica_groups=mesh['sub_0'=4,'sub_1'=4,'sub_2'=4,'sub_3'=2] {'sub_1'}, use_global_device_ids=true, to_apply=%region_2.0 | all-reduce | flops 1 | bytes 8 | tf_op jit(solution)/shard_map/psum | solution.py:42
  24.6 11.1 %psum.86 = f32[]{:T(128)} all-reduce(f32[]{:T(128)} %psum.85), channel_id=1, replica_groups=mesh['sub_0'=4,'sub_1'=4,'sub_2'=4,'sub_3'=2] {'sub_2'}, use_global_device_ids=true, to_apply=%region_3.0 | all-reduce | flops 1 | bytes 8 | tf_op jit(solution)/shard_map/psum | solution.py:42
  35.7 3.1 %psum.87 = f32[]{:T(128)} all-reduce(f32[]{:T(128)} %psum.86), channel_id=1, replica_groups=mesh['sub_0'=4,'sub_1'=4,'sub_2'=4,'sub_3'=2] {'sub_3'}, use_global_device_ids=true, to_apply=%region_4.0 | all-reduce | flops 1 | bytes 8 | tf_op jit(solution)/shard_map/psum | solution.py:42
  41.4 3.7 %collective-permute-done.1 = f32[32,64]{1,0:T(8,128)S(1)} collective-permute-done((f32[32,64]{1,0:T(8,128)S(1)}, f32[32,64]{1,0:T(8,128)S(1)}, u32[]{:S(2)}, u32[]{:S(2)}) %collective-permute-start.1) | collective-permute-done | bytes 8224 | tf_op jit(solution)/shard_map/ppermute | solution.py:37
  46.0 4.4 %collective-permute-done.2 = f32[32,64]{1,0:T(8,128)S(1)} collective-permute-done((f32[32,64]{1,0:T(8,128)S(1)}, f32[32,64]{1,0:T(8,128)S(1)}, u32[]{:S(2)}, u32[]{:S(2)}) %collective-permute-start.2) | collective-permute-done | bytes 8224 | tf_op jit(solution)/shard_map/ppermute | solution.py:37
  50.4 3.7 %collective-permute-done.3 = f32[32,64]{1,0:T(8,128)S(1)} collective-permute-done((f32[32,64]{1,0:T(8,128)S(1)}, f32[32,64]{1,0:T(8,128)S(1)}, u32[]{:S(2)}, u32[]{:S(2)}) %collective-permute-start.3) | collective-permute-done | bytes 8224 | tf_op jit(solution)/shard_map/ppermute | solution.py:37
  55.0 4.4 %collective-permute-done.4 = f32[32,64]{1,0:T(8,128)S(1)} collective-permute-done((f32[32,64]{1,0:T(8,128)S(1)}, f32[32,64]{1,0:T(8,128)S(1)}, u32[]{:S(2)}, u32[]{:S(2)}) %collective-permute-start.4) | collective-permute-done | bytes 8224 | tf_op jit(solution)/shard_map/ppermute | solution.py:37
  59.4 2.5 %collective-permute-start.5 = (f32[32,64]{1,0:T(8,128)S(1)}, f32[32,64]{1,0:T(8,128)S(1)}, u32[]{:S(2)}, u32[]{:S(2)}) collective-permute-start(f32[32,64]{1,0:T(8,128)S(1)} %add.254), channel_id=1, source_target_pairs={{0,32},{32,0},{1,33},{33,1},{2,34},{34,2},{3,35},{35,3},{4,36},{36... | collective-permute-start | bytes 24584 | tf_op jit(solution)/shard_map/ppermute | solution.py:37
  64.2 4.6 %collective-permute-done.6 = f32[32,64]{1,0:T(8,128)S(1)} collective-permute-done((f32[32,64]{1,0:T(8,128)S(1)}, f32[32,64]{1,0:T(8,128)S(1)}, u32[]{:S(2)}, u32[]{:S(2)}) %collective-permute-start.6) | collective-permute-done | bytes 8224 | tf_op jit(solution)/shard_map/ppermute | solution.py:37
  72.6 2.1 collective-permute-start.7
  74.7 2.4 %collective-permute-start.8 = (f32[1,128,512]{2,1,0:T(8,128)S(1)}, f32[1,128,512]{2,1,0:T(8,128)S(1)}, u32[]{:S(2)}, u32[]{:S(2)}) collective-permute-start(f32[1,128,512]{2,1,0:T(8,128)S(1)} %get-tuple-element.15), channel_id=1, source_target_pairs={{0,1},{1,2},{2,3},{3,4},{4,5},{5,6},{6,7},{7,8},{8,9},{9,10},{10,1... | collective-permute-start | bytes 786440 | tf_op jit(solution)/shard_map/ppermute | solution.py:21
  78.6 8.0 %collective-permute-done.8 = f32[1,128,512]{2,1,0:T(8,128)S(1)} collective-permute-done((f32[1,128,512]{2,1,0:T(8,128)S(1)}, f32[1,128,512]{2,1,0:T(8,128)S(1)}, u32[]{:S(2)}, u32[]{:S(2)}) %collective-permute-start.8) | collective-permute-done | bytes 262176 | tf_op jit(solution)/shard_map/ppermute | solution.py:21
  89.6 7.9 %psum.88 = f32[2]{0:T(128)S(1)} all-reduce(f32[2]{0:T(128)S(1)} %pad_maximum_fusion.6), channel_id=1, replica_groups=mesh['sub_0'=4,'sub_1'=4,'sub_2'=4,'sub_3'=2] {'sub_0'}, use_global_device_ids=true, to_apply=%region_8.9 | all-reduce | flops 2 | bytes 16 | tf_op jit(solution)/shard_map/psum | solution.py:42
  97.5 7.7 %psum.89 = f32[2]{0:T(128)S(1)} all-reduce(f32[2]{0:T(128)S(1)} %psum.88), channel_id=1, replica_groups=mesh['sub_0'=4,'sub_1'=4,'sub_2'=4,'sub_3'=2] {'sub_1'}, use_global_device_ids=true, to_apply=%region_9.10 | all-reduce | flops 2 | bytes 16 | tf_op jit(solution)/shard_map/psum | solution.py:42
  105.2 7.7 %psum.90 = f32[2]{0:T(128)S(1)} all-reduce(f32[2]{0:T(128)S(1)} %psum.89), channel_id=1, replica_groups=mesh['sub_0'=4,'sub_1'=4,'sub_2'=4,'sub_3'=2] {'sub_2'}, use_global_device_ids=true, to_apply=%region_10.11 | all-reduce | flops 2 | bytes 16 | tf_op jit(solution)/shard_map/psum | solution.py:42
  113.0 2.5 %psum.91 = f32[2]{0:T(128)S(1)} all-reduce(f32[2]{0:T(128)S(1)} %psum.90), channel_id=1, replica_groups=mesh['sub_0'=4,'sub_1'=4,'sub_2'=4,'sub_3'=2] {'sub_3'}, use_global_device_ids=true, to_apply=%region_11.12 | all-reduce | flops 2 | bytes 16 | tf_op jit(solution)/shard_map/psum | solution.py:42
  121.8 2.0 collective-permute-start.10
  127.0 3.8 %collective-permute-done.11 = f32[32,64]{1,0:T(8,128)S(1)} collective-permute-done((f32[32,64]{1,0:T(8,128)S(1)}, f32[32,64]{1,0:T(8,128)S(1)}, u32[]{:S(2)}, u32[]{:S(2)}) %collective-permute-start.11) | collective-permute-done | bytes 8224 | tf_op jit(solution)/shard_map/ppermute | solution.py:37
  136.0 3.8 %collective-permute-done.13 = f32[32,64]{1,0:T(8,128)S(1)} collective-permute-done((f32[32,64]{1,0:T(8,128)S(1)}, f32[32,64]{1,0:T(8,128)S(1)}, u32[]{:S(2)}, u32[]{:S(2)}) %collective-permute-start.13) | collective-permute-done | bytes 8224 | tf_op jit(solution)/shard_map/ppermute | solution.py:37
  144.6 4.2 %collective-permute-done.15 = f32[32,64]{1,0:T(8,128)S(1)} collective-permute-done((f32[32,64]{1,0:T(8,128)S(1)}, f32[32,64]{1,0:T(8,128)S(1)}, u32[]{:S(2)}, u32[]{:S(2)}) %collective-permute-start.15) | collective-permute-done | bytes 8224 | tf_op jit(solution)/shard_map/ppermute | solution.py:37
  150.6 3.2 %convolution_add_fusion = f32[4,128,512]{2,1,0:T(8,128)S(1)} fusion(f32[4,128,512]{2,1,0:T(8,128)} %get-tuple-element.8, f32[1,512,512]{2,1,0:T(8,128)S(1)} %copy-done, f32[128,512]{1,0:T(8,128)S(1)} %copy.10), kind=kOutput, calls=%fused_computation | convolution fusion | flops 1610874880 | bytes 3407872 | tf_op jit(solution)/shard_map/dot_general | solution.py:65
  153.9 2.1 collective-permute-start.16
  155.9 2.4 %collective-permute-start.17 = (f32[1,128,512]{2,1,0:T(8,128)S(1)}, f32[1,128,512]{2,1,0:T(8,128)S(1)}, u32[]{:S(2)}, u32[]{:S(2)}) collective-permute-start(f32[1,128,512]{2,1,0:T(8,128)S(1)} %get-tuple-element.12), channel_id=1, source_target_pairs={{0,1},{1,2},{2,3},{3,4},{4,5},{5,6},{6,7},{7,8},{8,9},{9,10},{10,1... | collective-permute-start | bytes 786440 | tf_op jit(solution)/shard_map/ppermute | solution.py:21
  159.8 8.0 %collective-permute-done.17 = f32[1,128,512]{2,1,0:T(8,128)S(1)} collective-permute-done((f32[1,128,512]{2,1,0:T(8,128)S(1)}, f32[1,128,512]{2,1,0:T(8,128)S(1)}, u32[]{:S(2)}, u32[]{:S(2)}) %collective-permute-start.17) | collective-permute-done | bytes 262176 | tf_op jit(solution)/shard_map/ppermute | solution.py:21
  171.5 7.7 %psum.92 = f32[3]{0:T(128)S(1)} all-reduce(f32[3]{0:T(128)S(1)} %pad_maximum_fusion.7), channel_id=1, replica_groups=mesh['sub_0'=4,'sub_1'=4,'sub_2'=4,'sub_3'=2] {'sub_0'}, use_global_device_ids=true, to_apply=%region_16.17 | all-reduce | flops 3 | bytes 24 | tf_op jit(solution)/shard_map/psum | solution.py:42
  179.9 9.5 %psum.93 = f32[3]{0:T(128)S(1)} all-reduce(f32[3]{0:T(128)S(1)} %psum.92), channel_id=1, replica_groups=mesh['sub_0'=4,'sub_1'=4,'sub_2'=4,'sub_3'=2] {'sub_1'}, use_global_device_ids=true, to_apply=%region_17.18 | all-reduce | flops 3 | bytes 24 | tf_op jit(solution)/shard_map/psum | solution.py:42
  189.4 7.7 %psum.94 = f32[3]{0:T(128)S(1)} all-reduce(f32[3]{0:T(128)S(1)} %psum.93), channel_id=1, replica_groups=mesh['sub_0'=4,'sub_1'=4,'sub_2'=4,'sub_3'=2] {'sub_2'}, use_global_device_ids=true, to_apply=%region_18.19 | all-reduce | flops 3 | bytes 24 | tf_op jit(solution)/shard_map/psum | solution.py:42
  197.1 2.5 %psum.95 = f32[3]{0:T(128)S(1)} all-reduce(f32[3]{0:T(128)S(1)} %psum.94), channel_id=1, replica_groups=mesh['sub_0'=4,'sub_1'=4,'sub_2'=4,'sub_3'=2] {'sub_3'}, use_global_device_ids=true, to_apply=%region_19.20 | all-reduce | flops 3 | bytes 24 | tf_op jit(solution)/shard_map/psum | solution.py:42
  207.5 5.1 %collective-permute-start.18 = (f32[1,128,512]{2,1,0:T(8,128)S(1)}, f32[1,128,512]{2,1,0:T(8,128)S(1)}, u32[]{:S(2)}, u32[]{:S(2)}) collective-permute-start(f32[1,128,512]{2,1,0:T(8,128)S(1)} %get-tuple-element.11), channel_id=1, source_target_pairs={{1,0},{2,1},{3,2},{4,3},{5,4},{6,5},{7,6},{8,7},{9,8},{10,9},{11,1... | collective-permute-start | bytes 786440 | tf_op jit(solution)/shard_map/ppermute | solution.py:23
  216.5 8.0 %collective-permute-done.19 = f32[1,128,512]{2,1,0:T(8,128)S(1)} collective-permute-done((f32[1,128,512]{2,1,0:T(8,128)S(1)}, f32[1,128,512]{2,1,0:T(8,128)S(1)}, u32[]{:S(2)}, u32[]{:S(2)}) %collective-permute-start.19) | collective-permute-done | bytes 262176 | tf_op jit(solution)/shard_map/ppermute | solution.py:21
  (84 shorter events, 46.4 us)
Async XLA Ops:
  0.6 70.0 %copy-start = (f32[1,512,512]{2,1,0:T(8,128)S(1)}, f32[1,512,512]{2,1,0:T(8,128)}, u32[]{:S(2)}) copy-start(f32[1,512,512]{2,1,0:T(8,128)} %param.10) | copy-start | bytes 3145732
  0.6 38.8 %copy-start.1 = (f32[4,128,512]{2,1,0:T(8,128)S(1)}, f32[4,128,512]{2,1,0:T(8,128)}, u32[]{:S(2)}) copy-start(f32[4,128,512]{2,1,0:T(8,128)} %param.7) | copy-start | bytes 3145732
  0.7 38.9 %copy-start.11 = (f32[512,64]{0,1:T(8,128)S(1)}, f32[512,64]{0,1:T(8,128)}, u32[]{:S(2)}) copy-start(f32[512,64]{0,1:T(8,128)} %param.12) | copy-start | bytes 393220
  2.9 37.1 %copy-start.12 = (f32[128,32]{0,1:T(8,128)S(1)}, f32[128,32]{0,1:T(8,128)}, u32[]{:S(2)}) copy-start(f32[128,32]{0,1:T(8,128)} %param.11) | copy-start | bytes 49156
  40.2 1.3 collective-permute-start
  41.4 3.7 %collective-permute-start.1 = (f32[32,64]{1,0:T(8,128)S(1)}, f32[32,64]{1,0:T(8,128)S(1)}, u32[]{:S(2)}, u32[]{:S(2)}) collective-permute-start(f32[32,64]{1,0:T(8,128)S(1)} %add.247), channel_id=1, source_target_pairs={{0,2},{2,0},{1,3},{3,1},{4,6},{6,4},{5,7},{7,5},{8,10},{10,8},{9,1... | collective-permute-start | bytes 24584 | tf_op jit(solution)/shard_map/ppermute | solution.py:37
  45.2 5.2 %collective-permute-start.2 = (f32[32,64]{1,0:T(8,128)S(1)}, f32[32,64]{1,0:T(8,128)S(1)}, u32[]{:S(2)}, u32[]{:S(2)}) collective-permute-start(f32[32,64]{1,0:T(8,128)S(1)} %add.248), channel_id=1, source_target_pairs={{0,4},{4,0},{1,5},{5,1},{2,6},{6,2},{3,7},{7,3},{8,12},{12,8},{9,1... | collective-permute-start | bytes 24584 | tf_op jit(solution)/shard_map/ppermute | solution.py:37
  50.4 3.7 %collective-permute-start.3 = (f32[32,64]{1,0:T(8,128)S(1)}, f32[32,64]{1,0:T(8,128)S(1)}, u32[]{:S(2)}, u32[]{:S(2)}) collective-permute-start(f32[32,64]{1,0:T(8,128)S(1)} %add.250), channel_id=1, source_target_pairs={{0,8},{8,0},{1,9},{9,1},{2,10},{10,2},{3,11},{11,3},{4,12},{12,4},... | collective-permute-start | bytes 24584 | tf_op jit(solution)/shard_map/ppermute | solution.py:37
  54.2 5.2 %collective-permute-start.4 = (f32[32,64]{1,0:T(8,128)S(1)}, f32[32,64]{1,0:T(8,128)S(1)}, u32[]{:S(2)}, u32[]{:S(2)}) collective-permute-start(f32[32,64]{1,0:T(8,128)S(1)} %add.252), channel_id=1, source_target_pairs={{0,16},{16,0},{1,17},{17,1},{2,18},{18,2},{3,19},{19,3},{4,20},{20... | collective-permute-start | bytes 24584 | tf_op jit(solution)/shard_map/ppermute | solution.py:37
  59.4 4.2 %collective-permute-start.5 = (f32[32,64]{1,0:T(8,128)S(1)}, f32[32,64]{1,0:T(8,128)S(1)}, u32[]{:S(2)}, u32[]{:S(2)}) collective-permute-start(f32[32,64]{1,0:T(8,128)S(1)} %add.254), channel_id=1, source_target_pairs={{0,32},{32,0},{1,33},{33,1},{2,34},{34,2},{3,35},{35,3},{4,36},{36... | collective-permute-start | bytes 24584 | tf_op jit(solution)/shard_map/ppermute | solution.py:37
  63.6 5.2 %collective-permute-start.6 = (f32[32,64]{1,0:T(8,128)S(1)}, f32[32,64]{1,0:T(8,128)S(1)}, u32[]{:S(2)}, u32[]{:S(2)}) collective-permute-start(f32[32,64]{1,0:T(8,128)S(1)} %add.256), channel_id=1, source_target_pairs={{0,64},{64,0},{1,65},{65,1},{2,66},{66,2},{3,67},{67,3},{4,68},{68... | collective-permute-start | bytes 24584 | tf_op jit(solution)/shard_map/ppermute | solution.py:37
  70.7 16.0 %copy-start.5 = (f32[4,128,512]{2,1,0:T(8,128)S(1)}, f32[4,128,512]{2,1,0:T(8,128)}, u32[]{:S(2)}) copy-start(f32[4,128,512]{2,1,0:T(8,128)} %param.8) | copy-start | bytes 3145732
  72.6 15.6 %copy-start.9 = (f32[4,128,512]{2,1,0:T(8,128)}, f32[4,128,512]{2,1,0:T(8,128)S(1)}, u32[]{:S(2)}) copy-start(f32[4,128,512]{2,1,0:T(8,128)S(1)} %convolution_add_fusion.1) | copy-start | bytes 3145732
  72.6 5.9 %collective-permute-start.7 = (f32[1,128,512]{2,1,0:T(8,128)S(1)}, f32[1,128,512]{2,1,0:T(8,128)S(1)}, u32[]{:S(2)}, u32[]{:S(2)}) collective-permute-start(f32[1,128,512]{2,1,0:T(8,128)S(1)} %get-tuple-element.14), channel_id=1, source_target_pairs={{1,0},{2,1},{3,2},{4,3},{5,4},{6,5},{7,6},{8,7},{9,8},{10,9},{11,1... | collective-permute-start | bytes 786440 | tf_op jit(solution)/shard_map/ppermute | solution.py:23
  74.7 11.9 %collective-permute-start.8 = (f32[1,128,512]{2,1,0:T(8,128)S(1)}, f32[1,128,512]{2,1,0:T(8,128)S(1)}, u32[]{:S(2)}, u32[]{:S(2)}) collective-permute-start(f32[1,128,512]{2,1,0:T(8,128)S(1)} %get-tuple-element.15), channel_id=1, source_target_pairs={{0,1},{1,2},{2,3},{3,4},{4,5},{5,6},{6,7},{7,8},{8,9},{9,10},{10,1... | collective-permute-start | bytes 786440 | tf_op jit(solution)/shard_map/ppermute | solution.py:21
  120.6 1.3 collective-permute-start.9
  121.8 3.7 %collective-permute-start.10 = (f32[32,64]{1,0:T(8,128)S(1)}, f32[32,64]{1,0:T(8,128)S(1)}, u32[]{:S(2)}, u32[]{:S(2)}) collective-permute-start(f32[32,64]{1,0:T(8,128)S(1)} %add.268), channel_id=1, source_target_pairs={{0,2},{2,0},{1,3},{3,1},{4,6},{6,4},{5,7},{7,5},{8,10},{10,8},{9,1... | collective-permute-start | bytes 24584 | tf_op jit(solution)/shard_map/ppermute | solution.py:37
  125.6 5.2 %collective-permute-start.11 = (f32[32,64]{1,0:T(8,128)S(1)}, f32[32,64]{1,0:T(8,128)S(1)}, u32[]{:S(2)}, u32[]{:S(2)}) collective-permute-start(f32[32,64]{1,0:T(8,128)S(1)} %add.269), channel_id=1, source_target_pairs={{0,4},{4,0},{1,5},{5,1},{2,6},{6,2},{3,7},{7,3},{8,12},{12,8},{9,1... | collective-permute-start | bytes 24584 | tf_op jit(solution)/shard_map/ppermute | solution.py:37
  130.8 3.7 %collective-permute-start.12 = (f32[32,64]{1,0:T(8,128)S(1)}, f32[32,64]{1,0:T(8,128)S(1)}, u32[]{:S(2)}, u32[]{:S(2)}) collective-permute-start(f32[32,64]{1,0:T(8,128)S(1)} %add.271), channel_id=1, source_target_pairs={{0,8},{8,0},{1,9},{9,1},{2,10},{10,2},{3,11},{11,3},{4,12},{12,4},... | collective-permute-start | bytes 24584 | tf_op jit(solution)/shard_map/ppermute | solution.py:37
  134.6 5.2 %collective-permute-start.13 = (f32[32,64]{1,0:T(8,128)S(1)}, f32[32,64]{1,0:T(8,128)S(1)}, u32[]{:S(2)}, u32[]{:S(2)}) collective-permute-start(f32[32,64]{1,0:T(8,128)S(1)} %add.273), channel_id=1, source_target_pairs={{0,16},{16,0},{1,17},{17,1},{2,18},{18,2},{3,19},{19,3},{4,20},{20... | collective-permute-start | bytes 24584 | tf_op jit(solution)/shard_map/ppermute | solution.py:37
  139.8 3.7 %collective-permute-start.14 = (f32[32,64]{1,0:T(8,128)S(1)}, f32[32,64]{1,0:T(8,128)S(1)}, u32[]{:S(2)}, u32[]{:S(2)}) collective-permute-start(f32[32,64]{1,0:T(8,128)S(1)} %add.275), channel_id=1, source_target_pairs={{0,32},{32,0},{1,33},{33,1},{2,34},{34,2},{3,35},{35,3},{4,36},{36... | collective-permute-start | bytes 24584 | tf_op jit(solution)/shard_map/ppermute | solution.py:37
  143.6 5.2 %collective-permute-start.15 = (f32[32,64]{1,0:T(8,128)S(1)}, f32[32,64]{1,0:T(8,128)S(1)}, u32[]{:S(2)}, u32[]{:S(2)}) collective-permute-start(f32[32,64]{1,0:T(8,128)S(1)} %add.277), channel_id=1, source_target_pairs={{0,64},{64,0},{1,65},{65,1},{2,66},{66,2},{3,67},{67,3},{4,68},{68... | collective-permute-start | bytes 24584 | tf_op jit(solution)/shard_map/ppermute | solution.py:37
  150.6 17.3 %copy-start.6 = (f32[4,128,512]{2,1,0:T(8,128)S(1)}, f32[4,128,512]{2,1,0:T(8,128)}, u32[]{:S(2)}) copy-start(f32[4,128,512]{2,1,0:T(8,128)} %param.8) | copy-start | bytes 3145732
  150.6 17.3 %copy-start.8 = (f32[4,128,512]{2,1,0:T(8,128)S(1)}, f32[4,128,512]{2,1,0:T(8,128)}, u32[]{:S(2)}) copy-start(f32[4,128,512]{2,1,0:T(8,128)} %get-tuple-element.8) | copy-start | bytes 3145732
  153.8 14.0 %copy-start.3 = (f32[4,128,512]{2,1,0:T(8,128)S(1)}, f32[4,128,512]{2,1,0:T(8,128)}, u32[]{:S(2)}) copy-start(f32[4,128,512]{2,1,0:T(8,128)} %param.9) | copy-start | bytes 3145732
  153.9 5.9 %collective-permute-start.16 = (f32[1,128,512]{2,1,0:T(8,128)S(1)}, f32[1,128,512]{2,1,0:T(8,128)S(1)}, u32[]{:S(2)}, u32[]{:S(2)}) collective-permute-start(f32[1,128,512]{2,1,0:T(8,128)S(1)} %get-tuple-element.13), channel_id=1, source_target_pairs={{1,0},{2,1},{3,2},{4,3},{5,4},{6,5},{7,6},{8,7},{9,8},{10,9},{11,1... | collective-permute-start | bytes 786440 | tf_op jit(solution)/shard_map/ppermute | solution.py:23
  155.9 11.9 %collective-permute-start.17 = (f32[1,128,512]{2,1,0:T(8,128)S(1)}, f32[1,128,512]{2,1,0:T(8,128)S(1)}, u32[]{:S(2)}, u32[]{:S(2)}) collective-permute-start(f32[1,128,512]{2,1,0:T(8,128)S(1)} %get-tuple-element.12), channel_id=1, source_target_pairs={{0,1},{1,2},{2,3},{3,4},{4,5},{5,6},{6,7},{7,8},{8,9},{9,10},{10,1... | collective-permute-start | bytes 786440 | tf_op jit(solution)/shard_map/ppermute | solution.py:21
  205.9 18.6 %copy-start.7 = (f32[4,128,512]{2,1,0:T(8,128)S(1)}, f32[4,128,512]{2,1,0:T(8,128)}, u32[]{:S(2)}) copy-start(f32[4,128,512]{2,1,0:T(8,128)} %param.8) | copy-start | bytes 3145732
  207.5 19.0 %copy-start.10 = (f32[4,128,512]{2,1,0:T(8,128)}, f32[4,128,512]{2,1,0:T(8,128)S(1)}, u32[]{:S(2)}) copy-start(f32[4,128,512]{2,1,0:T(8,128)S(1)} %multiply_add_fusion) | copy-start | bytes 3145732
  207.5 17.1 %copy-start.4 = (f32[4,128,512]{2,1,0:T(8,128)S(1)}, f32[4,128,512]{2,1,0:T(8,128)}, u32[]{:S(2)}) copy-start(f32[4,128,512]{2,1,0:T(8,128)} %param.9) | copy-start | bytes 3145732
  207.5 9.0 %collective-permute-start.18 = (f32[1,128,512]{2,1,0:T(8,128)S(1)}, f32[1,128,512]{2,1,0:T(8,128)S(1)}, u32[]{:S(2)}, u32[]{:S(2)}) collective-permute-start(f32[1,128,512]{2,1,0:T(8,128)S(1)} %get-tuple-element.11), channel_id=1, source_target_pairs={{1,0},{2,1},{3,2},{4,3},{5,4},{6,5},{7,6},{8,7},{9,8},{10,9},{11,1... | collective-permute-start | bytes 786440 | tf_op jit(solution)/shard_map/ppermute | solution.py:23
  212.6 11.9 %collective-permute-start.19 = (f32[1,128,512]{2,1,0:T(8,128)S(1)}, f32[1,128,512]{2,1,0:T(8,128)S(1)}, u32[]{:S(2)}, u32[]{:S(2)}) collective-permute-start(f32[1,128,512]{2,1,0:T(8,128)S(1)} %get-tuple-element.10), channel_id=1, source_target_pairs={{0,1},{1,2},{2,3},{3,4},{4,5},{5,6},{6,7},{7,8},{8,9},{9,10},{10,1... | collective-permute-start | bytes 786440 | tf_op jit(solution)/shard_map/ppermute | solution.py:21
  (1 other events, 14.0 us)
where the time goes:
time: 227 us; the launch traced here: 226 us
  blocking collectives  89.1 us (39%)
  waiting for transfers between devices  70.8 us (31%)
  starting transfers between devices  31 us (14%)
  other arithmetic  14.4 us (6%)
  between operations  10.1 us (4%)
  matrix products  9.41 us (4%)
    psum x12, blocking collectives, one_axis_at_a_time(): shard = lax.psum(shard, axis)  89.1 us
    ppermute x14, waiting for transfers between devices, swapped(): return lax.ppermute(block, axis, route)  41.8 us
    ppermute x3, waiting for transfers between devices, extended(): lax.ppermute(tail, axis, [(i, (i + 1) % count) for i in range(ends)])  24.1 us
    ppermute x14, starting transfers between devices, swapped(): return lax.ppermute(block, axis, route)  15.1 us
    ppermute x3, starting transfers between devices, extended(): lax.ppermute(head, axis, [((i + 1) % count, i) for i in range(ends)])  9.2 us
    ppermute x3, starting transfers between devices, extended(): lax.ppermute(tail, axis, [(i, (i + 1) % count) for i in range(ends)])  6.73 us
    dot_general x2, matrix products, precondition(): jnp.dot(field.reshape(layers * rows, depth), local_inverse[0], precision=...  5.1 us
    ppermute x3, waiting for transfers between devices, extended(): lax.ppermute(head, axis, [((i + 1) % count, i) for i in range(ends)])  4.85 us
  transfers between devices with their start and end apart: 20, of which 20 were waited for; matrix products, arithmetic and copies ran while one was open for 0% of the time, Pallas kernels for 0%

commit v1 on v0

v1 whole, which is shorter than its diff:
```python
import functools

import jax
import jax.numpy as jnp
from jax import lax
from jax.experimental import pallas as pl
from jax.experimental.pallas import tpu as pltpu
from jax.sharding import PartitionSpec as P

MESH = pl.DeviceIdType.MESH
F32 = jnp.float32
BF16 = jnp.bfloat16

CX, NY, NZ, KY, KZ, LEVELS = 4, 128, 512, 32, 64, 7
PK = 16
PAY = PK + 8
TOP = 8
PADY = NY + 2 * TOP


def split(x):
    high = x.astype(BF16)
    return high, (x - high.astype(F32)).astype(BF16)


def dot(a, b):
    return jnp.dot(a, b, preferred_element_type=F32)


def dot3(a, b):
    ah, al = a
    bh, bl = b
    return dot(ah, bh) + dot(al, bh) + dot(ah, bl)


def lanes(shape):
    return lax.broadcasted_iota(jnp.int32, shape, len(shape) - 1)


def pack(c):
    return jnp.where(lanes((PK, 128)) < KZ, c[:PK], c[PK:])


def masked(c):
    low = lanes((PK, 128)) < KZ
    return jnp.concatenate([jnp.where(low, c, 0.0), jnp.where(low, 0.0, c)], axis=0)


def neighbours_z(c):
    lane = lanes(c.shape)
    ahead = jnp.where(lane == NZ - 1, 0.0, pltpu.roll(c, NZ - 1, 1))
    behind = jnp.where(lane == 0, 0.0, pltpu.roll(c, 1, 1))
    return ahead + behind


def total(x):
    return jnp.sum(jnp.sum(x, axis=0, keepdims=True), axis=1, keepdims=True)


def fold(x):
    acc = x[0:8]
    for i in range(8, x.shape[0], 8):
        acc = acc + x[i : i + 8]
    return acc


def fold_lanes(x):
    return x[:, 0:128] + x[:, 128:256] + x[:, 256:384] + x[:, 384:512]


def kernel(
    r_h, sg_h, wd_h, mi_h, by_h, bz_h, gm_h,
    sol, res,
    R, SG, WD, MI, BY, BZ, GM,
    XB, MH, ML, L, LW, AL, W, Q, Z1, U2,
    BZH, BZL, TBH, TBL, B2H, B2L, BYH, BYL, BY2H, BY2L, BTH, BTL, GP,
    S3, G0, X, CS, SUM, PL,
    SND, RCV, CP, NBC, SC,
    ld_sem, snd_sem, rcv_sem, cps_sem, cpr_sem, hs_sem, hr_sem,
):
    b = lax.axis_index("sub")
    core = lax.rem(b, 2)
    cx = lax.rem(b // 2, 4)
    cz = lax.rem(b // 8, 4)
    cy = b // 32
    coords = (cx, cz, cy)
    strides = (2, 8, 32)
    mate = b + 1 - 2 * core
    far = b - 1 + 2 * core
    has_far = jnp.logical_and(far >= 0, far < 128)

    def peer(axis, d):
        c = coords[axis]
        return b + (lax.rem(c + d, 4) - c) * strides[axis]

    loads = [
        pltpu.make_async_copy(src, dst, ld_sem.at[i])
        for i, (src, dst) in enumerate(
            [(r_h, R), (by_h, BY), (bz_h, BZ), (mi_h.at[0], MI), (gm_h, GM), (sg_h, SG), (wd_h, WD)]
        )
    ]
    for c in loads:
        c.start()

    barrier = pltpu.get_barrier_semaphore()
    peers = [mate] + [peer(a, d) for a in range(3) for d in (1, 2, 3)]
    for p in peers:
        pl.semaphore_signal(barrier, inc=1, device_id=(p,), device_id_type=MESH)

    @pl.when(has_far)
    def _():
        pl.semaphore_signal(barrier, inc=1, device_id=(far,), device_id_type=MESH)

    loads[1].wait()
    loads[2].wait()
    by = BY[...]
    bz = BZ[...]
    bz2 = jnp.concatenate([bz, bz], axis=1)
    B2H[...], B2L[...] = split(bz2)
    BTH[...], BTL[...] = split(by.T)

    def project(field):
        half = dot3(split(field), (B2H[...], B2L[...]))
        return pack(dot3((BTH[...], BTL[...]), split(half)))

    loads[0].wait()
    acc = jnp.zeros((8, NZ), F32)
    for y in range(0, NY, 16):
        s = jnp.zeros((16, NZ), F32)
        q = jnp.zeros((16, NZ), F32)
        for x in range(CX):
            v = R[x, y : y + 16]
            s = s + v
            q = q + v * v
        X[y : y + 16] = s
        acc = acc + fold(q)
    SND[0, 0, :PK] = project(X[...])
    SND[0, 0, PK:] = fold_lanes(acc)

    pl.semaphore_wait(barrier, len(peers) + has_far.astype(jnp.int32))

    sends = []

    def send(src, dst, ss, rs, device):
        c = pltpu.make_async_remote_copy(
            src_ref=src, dst_ref=dst, send_sem=ss, recv_sem=rs, device_id=(device,), device_id_type=MESH
        )
        c.start()
        return c

    def to_mate(k, rows):
        c = send(SND.at[k, 0, rows], RCV.at[k, 0, rows], snd_sem.at[k, 0], rcv_sem.at[k, 0], mate)
        sends.append(c)
        return c

    def to_axis(k, axis, rows):
        cs = []
        for d in (1, 2, 3):
            i = 1 + 3 * axis + d - 1
            cs.append(
                send(SND.at[k, 1 + axis, rows], RCV.at[k, i, rows], snd_sem.at[k, i], rcv_sem.at[k, i], peer(axis, d))
            )
        sends.extend(cs)
        return cs

    def axis_sums(k, axis, rows):
        base = 1 + 3 * axis
        odd = lax.rem(coords[axis], 2)
        own = SND[k, 1 + axis, rows] + RCV[k, base + 2 - 2 * odd, rows]
        other = RCV[k, base + 1, rows] + RCV[k, base + 2 * odd, rows]
        return own, other, own + other

    ALLR = pl.ds(0, PAY)
    PKR = pl.ds(0, PK)
    SCR = pl.ds(PK, 8)

    def edges(k, field):
        send_mate = send(
            field.at[4 - 3 * core, TOP : TOP + NY], field.at[5 * core, TOP : TOP + NY],
            hs_sem.at[k, 0], hr_sem.at[k, 0], mate,
        )
        sends.append(send_mate)

        @pl.when(has_far)
        def _():
            send(
                field.at[1 + 3 * core, TOP : TOP + NY], field.at[5 - 5 * core, TOP : TOP + NY],
                hs_sem.at[k, 1], hr_sem.at[k, 1], far,
            )

    def edge_copy(k, field):
        return pltpu.make_async_remote_copy(
            src_ref=field.at[1 + 3 * core, TOP : TOP + NY], dst_ref=field.at[5 - 5 * core, TOP : TOP + NY],
            send_sem=hs_sem.at[k, 1], recv_sem=hr_sem.at[k, 1], device_id=(far,), device_id_type=MESH,
        )

    def mate_edge(k, field):
        return pltpu.make_async_remote_copy(
            src_ref=field.at[4 - 3 * core, TOP : TOP + NY], dst_ref=field.at[5 * core, TOP : TOP + NY],
            send_sem=hs_sem.at[k, 0], recv_sem=hr_sem.at[k, 0], device_id=(mate,), device_id_type=MESH,
        )

    def far_coarse(k):
        return pltpu.make_async_remote_copy(
            src_ref=CP.at[k], dst_ref=NBC.at[k, 1 - core],
            send_sem=cps_sem.at[k, 1], recv_sem=cpr_sem.at[k, 1], device_id=(far,), device_id_type=MESH,
        )

    def mate_coarse(k):
        return pltpu.make_async_remote_copy(
            src_ref=CP.at[k], dst_ref=NBC.at[k, core],
            send_sem=cps_sem.at[k, 0], recv_sem=cpr_sem.at[k, 0], device_id=(mate,), device_id_type=MESH,
        )

    def clear(field):
        zero = jnp.zeros((TOP, NZ), F32)
        for x in range(6):
            field[x, 0:TOP] = zero
            field[x, TOP + NY :] = zero

        @pl.when(jnp.logical_not(has_far))
        def _():
            field[5 * core, TOP : TOP + NY] = jnp.zeros((NY, NZ), F32)

    def local_pair(first, second, src, field):
        for at, x in ((0, first), (NY, second)):
            high, low = split(src[x])
            XB[at : at + NY, 0:NZ] = high
            XB[at : at + NY, NZ:] = low
        high = XB[:, 0:NZ]
        low = XB[:, NZ:]
        out = dot(high, MH[...]) + dot(low, MH[...]) + dot(high, ML[...])
        field[first + 1, TOP : TOP + NY] = out[:NY]
        field[second + 1, TOP : TOP + NY] = out[NY:]

    def operator(field, out):
        for y in range(0, NY, 16):
            layer_sum = jnp.zeros((16, NZ), F32)
            lo = TOP + y
            for x in range(CX):
                c = field[x + 1, lo : lo + 16]
                up = field[x + 2, lo : lo + 16]
                dn = field[x, lo : lo + 16]
                beside = field[x + 1, lo + 1 : lo + 17] + field[x + 1, lo - 1 : lo + 15] + neighbours_z(c)
                value = (6.0 + SG[x, y : y + 16]) * c - (up + dn + beside) + WD[x, y : y + 16] * (up - dn)
                out[x, y : y + 16] = value
                layer_sum = layer_sum + value
            SUM[y : y + 16] = layer_sum

    def coarse_start(k):
        pass

    def expand(own, low, high):
        cx3 = jnp.concatenate([masked(own), masked(low), masked(high)], axis=1)
        ch, cl = split(cx3)
        e = dot3((BYH[...], BYL[...]), (ch, cl))
        e2 = dot3((BY2H[...], BY2L[...]), (ch[:, :128], cl[:, :128]))
        rows = jnp.concatenate([e[:, 0:128], e[:, 128:256], e[:, 256:384]], axis=0)
        rh, rl = split(rows)
        S3[...] = dot3((rh, rl), (BZH[...], BZL[...]))
        eh, el = split(e2)
        G0[...] = dot3((eh, el), (BZH[...], BZL[...])) - dot3((rh[:NY], rl[:NY]), (TBH[...], TBL[...]))

    def spread_terms(x, y):
        s = S3[y : y + 16]
        sg = SG[x, y : y + 16]
        g = G0[y : y + 16]
        if x == 0:
            w0 = WD[0, y : y + 16]
            return g + (sg - 1.0 + w0) * s - (1.0 + w0) * S3[NY + y : NY + y + 16]
        if x == CX - 1:
            w3 = WD[CX - 1, y : y + 16]
            return g + (sg - 1.0 - w3) * s - (1.0 - w3) * S3[2 * NY + y : 2 * NY + y + 16]
        return g + (sg - 2.0) * s

    def coarse_finish(k):
        own, other, every = axis_sums(k, 2, ALLR)
        far_y = far // 32
        same = (far_y // 2) == (cy // 2)
        top = GP[6] * every[:PK]
        mine = CP[k] + GP[5] * own[:PK] + top
        mate_part = NBC[k, 1 - core] + GP[5] * own[:PK] + top
        far_part = NBC[k, core] + GP[5] * jnp.where(same, own[:PK], other[:PK]) + top
        far_part = jnp.where(has_far, far_part, 0.0)
        low = jnp.where(core == 0, far_part, mate_part)
        high = jnp.where(core == 0, mate_part, far_part)
        return mine, low, high, every

    def wait_coarse_neighbours(k):
        mate_coarse(k).wait_recv()

        @pl.when(has_far)
        def _():
            far_coarse(k).wait_recv()

    step = to_mate(0, ALLR)
    loads[3].wait()
    for y in range(0, NZ, 64):
        MH[y : y + 64], ML[y : y + 64] = split(MI[y : y + 64])
    loads[4].wait()
    for level in range(LEVELS):
        g = GM[level] * (1.0 / (CX * 2 ** (level + 1)) ** 0.5)
        GP[level] = jnp.concatenate([g[:PK], g[PK:]], axis=1)
    step.wait_recv()
    SND[0, 1] = SND[0, 0] + RCV[0, 0]
    CP[0] = GP[0] * SND[0, 1, :PK]
    steps = to_axis(0, 0, ALLR)
    local_pair(0, 3, R, L)
    edges(0, L)
    for c in steps:
        c.wait_recv()
    own, other, every = axis_sums(0, 0, ALLR)
    SND[0, 2] = every
    steps = to_axis(0, 1, ALLR)
    CP[0] += GP[1] * own[:PK] + GP[2] * every[:PK]
    local_pair(1, 2, R, L)
    clear(L)
    for c in steps:
        c.wait_recv()
    own, other, every = axis_sums(0, 1, ALLR)
    SND[0, 3] = every
    steps = to_axis(0, 2, ALLR)
    CP[0] += GP[3] * own[:PK] + GP[4] * every[:PK]
    mate_coarse(0).start()

    @pl.when(has_far)
    def _():
        far_coarse(0).start()

    bzt = bz2.T
    BZH[...], BZL[...] = split(bzt)
    TBH[...], TBL[...] = split(neighbours_z(bzt))
    BYH[...], BYL[...] = split(by)
    zero = jnp.zeros((1, KY), F32)
    by2 = 6.0 * by - jnp.concatenate([by[1:], zero], axis=0) - jnp.concatenate([zero, by[:-1]], axis=0)
    BY2H[...], BY2L[...] = split(by2)
    loads[5].wait()
    loads[6].wait()
    for y in range(0, NY, 16):
        ssum = SG[0, y : y + 16] + SG[1, y : y + 16] + SG[2, y : y + 16] + SG[3, y : y + 16]
        CS[y : y + 16] = ssum + WD[0, y : y + 16] - WD[3, y : y + 16] - 6.0

    mate_edge(0, L).wait_recv()

    @pl.when(has_far)
    def _():
        edge_copy(0, L).wait_recv()

    operator(L, AL)
    PL[...] = project(SUM[...])
    for c in steps:
        c.wait_recv()
    wait_coarse_neighbours(0)
    mine, low, high, every = coarse_finish(0)
    rr = total(every[PK:])
    expand(mine, low, high)
    for y in range(0, NY, 16):
        s = S3[y : y + 16]
        w0 = WD[0, y : y + 16]
        w3 = WD[3, y : y + 16]
        X[y : y + 16] = (
            4.0 * G0[y : y + 16] + CS[y : y + 16] * s
            - (1.0 + w0) * S3[NY + y : NY + y + 16] - (1.0 - w3) * S3[2 * NY + y : 2 * NY + y + 16]
        )
    SND[1, 0, :PK] = PL[...] + project(X[...])

    step = to_mate(1, PKR)
    beta = jnp.sqrt(rr)
    inv = 1.0 / beta

    def build_w(x):
        for y in range(0, NY, 16):
            W[x, y : y + 16] = (AL[x, y : y + 16] + spread_terms(x, y)) * inv

    build_w(0)
    build_w(3)
    step.wait_recv()
    SND[1, 1, :PK] = SND[1, 0, :PK] + RCV[1, 0, :PK]
    CP[1] = GP[0] * SND[1, 1, :PK]
    steps = to_axis(1, 0, PKR)
    local_pair(0, 3, W, LW)
    edges(1, LW)
    build_w(1)
    build_w(2)
    for c in steps:
        c.wait_recv()
    own, other, every = axis_sums(1, 0, PKR)
    SND[1, 2, :PK] = every
    steps = to_axis(1, 1, PKR)
    CP[1] += GP[1] * own + GP[2] * every
    local_pair(1, 2, W, LW)
    clear(LW)
    for c in steps:
        c.wait_recv()
    own, other, every = axis_sums(1, 1, PKR)
    SND[1, 3, :PK] = every
    steps = to_axis(1, 2, PKR)
    CP[1] += GP[3] * own + GP[4] * every
    mate_coarse(1).start()

    @pl.when(has_far)
    def _():
        far_coarse(1).start()

    for x in range(CX):
        for y in range(0, NY, 16):
            Z1[x, y : y + 16] = (L[x + 1, TOP + y : TOP + y + 16] + S3[y : y + 16]) * inv
    vw = jnp.zeros((8, NZ), F32)
    ww = jnp.zeros((8, NZ), F32)
    for x in range(CX):
        for y in range(0, NY, 16):
            w = W[x, y : y + 16]
            vw = vw + fold(R[x, y : y + 16] * w)
            ww = ww + fold(w * w)
    vw = fold_lanes(vw) * inv
    ww = fold_lanes(ww)

    mate_edge(1, LW).wait_recv()

    @pl.when(has_far)
    def _():
        edge_copy(1, LW).wait_recv()

    operator(LW, Q)
    for c in steps:
        c.wait_recv()
    wait_coarse_neighbours(1)
    mine, low, high, _every = coarse_finish(1)
    expand(mine * inv, low * inv, high * inv)
    vq = jnp.zeros((8, NZ), F32)
    wq = jnp.zeros((8, NZ), F32)
    qq = jnp.zeros((8, NZ), F32)
    for x in range(CX):
        for y in range(0, NY, 16):
            q = Q[x, y : y + 16] + spread_terms(x, y)
            Q[x, y : y + 16] = q
            vq = vq + fold(R[x, y : y + 16] * q)
            wq = wq + fold(W[x, y : y + 16] * q)
            qq = qq + fold(q * q)
    row = lax.broadcasted_iota(jnp.int32, (8, 128), 0)
    parts = jnp.zeros((8, 128), F32)
    for i, part in enumerate((vw, ww, fold_lanes(vq) * inv, fold_lanes(wq), fold_lanes(qq))):
        parts = jnp.where(row == i, jnp.sum(part, axis=0, keepdims=True), parts)
    SC[0] = parts

    SND[2, 0, PK:] = parts
    step = to_mate(2, SCR)
    for x in range(CX):
        for y in range(0, NY, 16):
            U2[x, y : y + 16] = LW[x + 1, TOP + y : TOP + y + 16] + S3[y : y + 16]
    step.wait_recv()
    SND[2, 1, PK:] = SND[2, 0, PK:] + RCV[2, 0, PK:]
    for axis in range(3):
        for c in to_axis(2, axis, SCR):
            c.wait_recv()
        _own, _other, every = axis_sums(2, axis, SCR)
        if axis < 2:
            SND[2, 2 + axis, PK:] = every
    sums = jnp.sum(every, axis=1, keepdims=True)
    h11, gww, gvq, gwq, gqq = [sums[i : i + 1] for i in range(5)]
    rho = gwq / gww
    qhat = gqq / gww
    scale = beta / gww / (qhat - rho * rho)
    one = scale * (qhat * h11 - rho * gvq)
    two = scale * (gvq - rho * h11)
    for x in range(CX):
        for y in range(0, NY, 16):
            sol[x, y : y + 16] = one * Z1[x, y : y + 16] + two * U2[x, y : y + 16]
            res[x, y : y + 16] = R[x, y : y + 16] - one * W[x, y : y + 16] - two * Q[x, y : y + 16]

    for c in sends:
        c.wait_send()
    for k in range(2):
        mate_coarse(k).wait_send()

    @pl.when(has_far)
    def _():
        for k in range(2):
            far_coarse(k).wait_send()
        edge_copy(0, L).wait_send()
        edge_copy(1, LW).wait_send()


def on_device(right_side, sigma, wind, local_inverse, basis_y, basis_z, gamma):
    field = jax.ShapeDtypeStruct((CX, NY, NZ), F32)
    v = pltpu.VMEM
    dma = pltpu.SemaphoreType.DMA
    block = (CX, NY, NZ)
    return pl.pallas_call(
        kernel,
        out_shape=(field, field),
        in_specs=[pl.BlockSpec(memory_space=pl.ANY)] * 7,
        out_specs=[pl.BlockSpec(memory_space=pltpu.VMEM)] * 2,
        scratch_shapes=[
            v(block, F32), v(block, F32), v(block, F32), v((NZ, NZ), F32), v((NY, KY), F32), v((NZ, KZ), F32),
            v((LEVELS, KY, KZ), F32),
            v((2 * NY, 2 * NZ), BF16), v((NZ, NZ), BF16), v((NZ, NZ), BF16),
            v((6, PADY, NZ), F32), v((6, PADY, NZ), F32), v(block, F32), v(block, F32), v(block, F32), v(block, F32),
            v(block, F32),
            v((128, NZ), BF16), v((128, NZ), BF16), v((128, NZ), BF16), v((128, NZ), BF16),
            v((NZ, 128), BF16), v((NZ, 128), BF16),
            v((NY, KY), BF16), v((NY, KY), BF16), v((NY, KY), BF16), v((NY, KY), BF16),
            v((KY, NY), BF16), v((KY, NY), BF16), v((LEVELS, PK, 128), F32),
            v((3 * NY, NZ), F32), v((NY, NZ), F32), v((NY, NZ), F32), v((NY, NZ), F32), v((NY, NZ), F32),
            v((PK, 128), F32),
            v((3, 4, PAY, 128), F32), v((3, 10, PAY, 128), F32), v((2, PK, 128), F32), v((2, 2, PK, 128), F32),
            v((1, 8, 128), F32),
            dma((7,)), dma((3, 10)), dma((3, 10)), dma((2, 2)), dma((2, 2)), dma((2, 2)), dma((2, 2)),
        ],
        compiler_params=pltpu.CompilerParams(
            collective_id=0, has_side_effects=True, vmem_limit_bytes=48 * 1024 * 1024
        ),
    )(right_side, sigma, wind, local_inverse, basis_y, basis_z, gamma)


def solution(mesh):
    row = P("sub", None, None)
    in_specs = (row, row, row, row, P(), P(), P())
    return jax.shard_map(on_device, mesh=mesh, in_specs=in_specs, out_specs=(row, row), check_vma=False)
```

time: 227 us -> 56.1 us (0.25)
  the two profiles are of different devices: /device:TPU:8 before, /device:TPU:0 now
where the time goes in v1:
time: 56.1 us; the launch traced here: 55.8 us
  Pallas kernels  47.6 us (85%)
  local copies, waits for them, and re-layouts  7.49 us (13%)
  between operations  0.67 us (1%)
    pallas_call x1, Pallas kernels, on_device(): pl.pallas_call(kernel, out_shape=(field, field), in_specs=[pl.BlockSpec(m...  47.6 us
    unnamed x12, local copies, waits for them, and re-layouts  7.49 us

profile of v1, /device:TPU:0, one launch (start us, length us, event | category | flops | bytes accessed | tf_op | source)
XLA Modules:
  0.0 55.8 jit_solution(17030195910130785201)
XLA Ops:
  0.6 0.8 %copy.9.by_h = f32[128,32]{1,0:T(8,128)S(1)} copy(f32[128,32]{0,1:T(8,128)} %param.11) | data formatting | bytes 32768 | tf_op args[4]
  1.4 0.0 copy-start.3
  1.5 1.1 %copy.10.bz_h = f32[512,64]{1,0:T(8,128)S(1)} copy(f32[512,64]{0,1:T(8,128)} %param.12) | data formatting | bytes 262144 | tf_op args[5]
  2.5 0.0 copy-done.3
  2.5 0.0 copy-start
  2.5 1.2 %copy-done = f32[4,128,512]{2,1,0:T(8,128)S(1)} copy-done((f32[4,128,512]{2,1,0:T(8,128)S(1)}, f32[4,128,512]{2,1,0:T(8,128)}, u32[]{:S(2)}) %copy-start) | copy-done | bytes 1048600
  3.8 0.0 copy-start.1
  3.8 1.2 %copy-done.1 = f32[4,128,512]{2,1,0:T(8,128)S(1)} copy-done((f32[4,128,512]{2,1,0:T(8,128)S(1)}, f32[4,128,512]{2,1,0:T(8,128)}, u32[]{:S(2)}) %copy-start.1) | copy-done | bytes 1048600
  5.0 0.0 copy-start.2
  5.0 1.2 %copy-done.2 = f32[4,128,512]{2,1,0:T(8,128)S(1)} copy-done((f32[4,128,512]{2,1,0:T(8,128)S(1)}, f32[4,128,512]{2,1,0:T(8,128)}, u32[]{:S(2)}) %copy-start.2) | copy-done | bytes 1048600
  6.2 47.6 %shard_map.86 = (f32[4,128,512]{2,1,0:T(8,128)S(1)}, f32[4,128,512]{2,1,0:T(8,128)S(1)}) custom-call(f32[4,128,512]{2,1,0:T(8,128)S(1)} %copy-done, f32[4,128,512]{2,1,0:T(8,128)S(1)} %copy-done.1, f32[4,128,512]{2,1,0:T(8,128)S(1)} %copy-done.2, f32[1,512,512]{2,1,0:T(8,128)} %mi_h.1, f32[128,32]{1,0:T(8,128)S(1)} %copy.9.by_h, f32[512,64]{1,0:T(8,128)S(1)} %copy.10.bz_h, ...), custom_call_target="tpu_custom_call" | custom-call | tf_op jit(solution)/shard_map/pallas_call | solution.py:489
  53.9 1.0 %copy.13 = f32[4,128,512]{2,1,0:T(8,128)} copy(f32[4,128,512]{2,1,0:T(8,128)S(1)} %get-tuple-element.4) | data formatting | bytes 2097152
  54.8 1.0 %copy.14 = f32[4,128,512]{2,1,0:T(8,128)} copy(f32[4,128,512]{2,1,0:T(8,128)S(1)} %get-tuple-element.5) | data formatting | bytes 2097152
Async XLA Ops:
  1.4 1.1 %copy-start.3 = (f32[7,32,64]{2,1,0:T(8,128)S(1)}, f32[7,32,64]{2,1,0:T(8,128)}, u32[]{:S(2)}) copy-start(f32[7,32,64]{2,1,0:T(8,128)} %gm_h.1) | copy-start | bytes 172036
  2.5 1.2 %copy-start = (f32[4,128,512]{2,1,0:T(8,128)S(1)}, f32[4,128,512]{2,1,0:T(8,128)}, u32[]{:S(2)}) copy-start(f32[4,128,512]{2,1,0:T(8,128)} %r_h.1) | copy-start | bytes 3145732
  3.8 1.2 %copy-start.1 = (f32[4,128,512]{2,1,0:T(8,128)S(1)}, f32[4,128,512]{2,1,0:T(8,128)}, u32[]{:S(2)}) copy-start(f32[4,128,512]{2,1,0:T(8,128)} %sg_h.1) | copy-start | bytes 3145732
  5.0 1.2 %copy-start.2 = (f32[4,128,512]{2,1,0:T(8,128)S(1)}, f32[4,128,512]{2,1,0:T(8,128)}, u32[]{:S(2)}) copy-start(f32[4,128,512]{2,1,0:T(8,128)} %wd_h.1) | copy-start | bytes 3145732

commit v2 on v1

--- a/solution.py
+++ b/solution.py
@@ -70,12 +70,12 @@
 
 def kernel(
     r_h, sg_h, wd_h, mi_h, by_h, bz_h, gm_h,
-    sol, res,
-    R, SG, WD, MI, BY, BZ, GM,
-    XB, MH, ML, L, LW, AL, W, Q, Z1, U2,
+    R, W, Q, Z1, U2, AB,
+    SG, WD, MI, BY, BZ, GM,
+    XB, MH, ML, L, LW, AL,
     BZH, BZL, TBH, TBL, B2H, B2L, BYH, BYL, BY2H, BY2L, BTH, BTL, GP,
     S3, G0, X, CS, SUM, PL,
-    SND, RCV, CP, NBC, SC,
+    SND, RCV, CP, NBC,
     ld_sem, snd_sem, rcv_sem, cps_sem, cpr_sem, hs_sem, hr_sem,
 ):
     b = lax.axis_index("sub")
@@ -113,11 +113,11 @@
 
     loads[1].wait()
     loads[2].wait()
-    by = BY[...]
+    by_t = BY[...]
     bz = BZ[...]
-    bz2 = jnp.concatenate([bz, bz], axis=1)
-    B2H[...], B2L[...] = split(bz2)
-    BTH[...], BTL[...] = split(by.T)
+    bzt = jnp.concatenate([bz, bz], axis=0)
+    B2H[...], B2L[...] = split(bzt.T)
+    BTH[...], BTL[...] = split(by_t)
 
     def project(field):
         half = dot3(split(field), (B2H[...], B2L[...]))
@@ -246,9 +246,6 @@
                 out[x, y : y + 16] = value
                 layer_sum = layer_sum + value
             SUM[y : y + 16] = layer_sum
-
-    def coarse_start(k):
-        pass
 
     def expand(own, low, high):
         cx3 = jnp.concatenate([masked(own), masked(low), masked(high)], axis=1)
@@ -327,7 +324,7 @@
     def _():
         far_coarse(0).start()
 
-    bzt = bz2.T
+    by = by_t.T
     BZH[...], BZL[...] = split(bzt)
     TBH[...], TBL[...] = split(neighbours_z(bzt))
     BYH[...], BYL[...] = split(by)
@@ -441,7 +438,6 @@
     parts = jnp.zeros((8, 128), F32)
     for i, part in enumerate((vw, ww, fold_lanes(vq) * inv, fold_lanes(wq), fold_lanes(qq))):
         parts = jnp.where(row == i, jnp.sum(part, axis=0, keepdims=True), parts)
-    SC[0] = parts
 
     SND[2, 0, PK:] = parts
     step = to_mate(2, SCR)
@@ -463,10 +459,7 @@
     scale = beta / gww / (qhat - rho * rho)
     one = scale * (qhat * h11 - rho * gvq)
     two = scale * (gvq - rho * h11)
-    for x in range(CX):
-        for y in range(0, NY, 16):
-            sol[x, y : y + 16] = one * Z1[x, y : y + 16] + two * U2[x, y : y + 16]
-            res[x, y : y + 16] = R[x, y : y + 16] - one * W[x, y : y + 16] - two * Q[x, y : y + 16]
+    AB[...] = jnp.where(row == 0, one, two)
 
     for c in sends:
         c.wait_send()
@@ -481,22 +474,37 @@
         edge_copy(1, LW).wait_send()
 
 
+def combine(R, W, Q, Z1, U2, AB, sol_h, res_h, SOL, RES, sem):
+    one = AB[0:1, 0:1]
+    two = AB[1:2, 0:1]
+    copies = []
+    for x in range(CX):
+        for y in range(0, NY, 16):
+            SOL[x, y : y + 16] = one * Z1[x, y : y + 16] + two * U2[x, y : y + 16]
+            RES[x, y : y + 16] = R[x, y : y + 16] - one * W[x, y : y + 16] - two * Q[x, y : y + 16]
+        for i, (src, dst) in enumerate(((SOL, sol_h), (RES, res_h))):
+            c = pltpu.make_async_copy(src.at[x], dst.at[x], sem.at[2 * x + i])
+            c.start()
+            copies.append(c)
+    for c in copies:
+        c.wait()
+
+
 def on_device(right_side, sigma, wind, local_inverse, basis_y, basis_z, gamma):
     field = jax.ShapeDtypeStruct((CX, NY, NZ), F32)
     v = pltpu.VMEM
     dma = pltpu.SemaphoreType.DMA
     block = (CX, NY, NZ)
-    return pl.pallas_call(
+    parts = pl.pallas_call(
         kernel,
-        out_shape=(field, field),
-        in_specs=[pl.BlockSpec(memory_space=pl.ANY)] * 7,
-        out_specs=[pl.BlockSpec(memory_space=pltpu.VMEM)] * 2,
+        out_shape=(field,) * 5 + (jax.ShapeDtypeStruct((8, 128), F32),),
+        in_specs=[pl.BlockSpec(memory_space=pltpu.HBM)] * 7,
+        out_specs=[pl.BlockSpec(memory_space=pltpu.VMEM)] * 6,
         scratch_shapes=[
-            v(block, F32), v(block, F32), v(block, F32), v((NZ, NZ), F32), v((NY, KY), F32), v((NZ, KZ), F32),
+            v(block, F32), v(block, F32), v((NZ, NZ), F32), v((KY, NY), F32), v((KZ, NZ), F32),
             v((LEVELS, KY, KZ), F32),
             v((2 * NY, 2 * NZ), BF16), v((NZ, NZ), BF16), v((NZ, NZ), BF16),
-            v((6, PADY, NZ), F32), v((6, PADY, NZ), F32), v(block, F32), v(block, F32), v(block, F32), v(block, F32),
-            v(block, F32),
+            v((6, PADY, NZ), F32), v((6, PADY, NZ), F32), v(block, F32),
             v((128, NZ), BF16), v((128, NZ), BF16), v((128, NZ), BF16), v((128, NZ), BF16),
             v((NZ, 128), BF16), v((NZ, 128), BF16),
             v((NY, KY), BF16), v((NY, KY), BF16), v((NY, KY), BF16), v((NY, KY), BF16),
@@ -504,13 +512,20 @@
             v((3 * NY, NZ), F32), v((NY, NZ), F32), v((NY, NZ), F32), v((NY, NZ), F32), v((NY, NZ), F32),
             v((PK, 128), F32),
             v((3, 4, PAY, 128), F32), v((3, 10, PAY, 128), F32), v((2, PK, 128), F32), v((2, 2, PK, 128), F32),
-            v((1, 8, 128), F32),
             dma((7,)), dma((3, 10)), dma((3, 10)), dma((2, 2)), dma((2, 2)), dma((2, 2)), dma((2, 2)),
         ],
         compiler_params=pltpu.CompilerParams(
-            collective_id=0, has_side_effects=True, vmem_limit_bytes=48 * 1024 * 1024
+            collective_id=0, has_side_effects=True, vmem_limit_bytes=40 * 1024 * 1024
         ),
-    )(right_side, sigma, wind, local_inverse, basis_y, basis_z, gamma)
+    )(*[pltpu.with_memory_space_constraint(t, pltpu.HBM) for t in (right_side, sigma, wind, local_inverse, basis_y.T, basis_z.T, gamma)])
+    return pl.pallas_call(
+        combine,
+        out_shape=(field, field),
+        in_specs=[pl.BlockSpec(memory_space=pltpu.VMEM)] * 6,
+        out_specs=[pl.BlockSpec(memory_space=pltpu.HBM)] * 2,
+        scratch_shapes=[v(block, F32), v(block, F32), dma((2 * CX,))],
+        compiler_params=pltpu.CompilerParams(vmem_limit_bytes=16 * 1024 * 1024),
+    )(*parts)
 
 
 def solution(mesh):

time: 56.1 us -> 49.6 us (0.88)
  local copies, waits for them, and re-layouts: 7.49 us -> 0 us
  Pallas kernels: 47.6 us -> 48.8 us
    unnamed x12 -> x0, local copies, waits for them, and re-layouts: 7.49 us -> none
    pallas_call x1 -> x2, Pallas kernels: 47.6 us -> 48.8 us  [the longest x1 47.4 us: on_device(): pl.pallas_call(kernel, out_shape=(field,) * 5 + (jax.ShapeDtypeStruct((8,...]
where the time goes in v2:
time: 49.6 us; the launch traced here: 49.5 us
  Pallas kernels  48.8 us (98%)
  between operations  0.64 us (1%)
    pallas_call x1, Pallas kernels, on_device(): pl.pallas_call(kernel, out_shape=(field,) * 5 + (jax.ShapeDtypeStruct((8,...  47.4 us
    pallas_call x1, Pallas kernels, on_device(): pl.pallas_call(combine, out_shape=(field, field), in_specs=[pl.BlockSpec(...  1.48 us

profile of v2, /device:TPU:0, one launch (start us, length us, event | category | flops | bytes accessed | tf_op | source)
XLA Modules:
  0.0 49.5 jit_solution(5371169111498777103)
XLA Ops:
  0.6 47.4 %shard_map.86 = (f32[4,128,512]{2,1,0:T(8,128)S(1)}, f32[4,128,512]{2,1,0:T(8,128)S(1)}, f32[4,128,512]{2,1,0:T(8,128)S(1)}, f32[4,128,512]{2,1,0:T(8,128)S(1)},...) custom-call(f32[4,128,512]{2,1,0:T(8,128)} %r_h.1, f32[4,128,512]{2,1,0:T(8,128)} %sg_h.1, f32[4,128,512]{2,1,0:T(8,128)} %wd_h.1, ...), custom_call_target="tpu_custom_call" | custom-call | tf_op jit(solution)/shard_map/pallas_call | solution.py:498
  48.0 1.5 %shard_map.87 = (f32[4,128,512]{2,1,0:T(8,128)}, f32[4,128,512]{2,1,0:T(8,128)}) custom-call(f32[4,128,512]{2,1,0:T(8,128)S(1)} %get-tuple-element.8.R, f32[4,128,512]{2,1,0:T(8,128)S(1)} %get-tuple-element.9.W, f32[4,128,512]{2,1,0:T(8,128)S(1)} %get-tuple-element.10.Q, f32[4,128,512]{2,1,0:T(8,128)S(1)} %get-tuple-element.11.Z1, ...), custom_call_target="tpu_custom_call" | custom-call | tf_op jit(solution)/shard_map/pallas_call | solution.py:521
